TPU v7x, 32 devices: a whole 2x2x4 slice. The times are simulated.
32 devices in a mesh: seq: 4 (over y, x), wshard: 8 (over z, core).
Axes of the slice: x: 2, y: 2, z: 4, core: 2. Of those that a mesh axis runs over, the one named last changes fastest.
Arguments:
- layer_input: bfloat16 [8, 1024, 1536], P('wshard', 'seq'), may hold values from -6 to 6
- lengths: int32 [8], P('wshard'), may hold values from 256 to 1024, as said below
- norm_attn: float32 [1536], replicated, may hold values from 0.1 to 1.9
- w_query: bfloat16 [1536, 1536], P('wshard'), may hold values from -0.15625 to 0.15625
- w_key: bfloat16 [1536, 1536], P('wshard'), may hold values from -0.15625 to 0.15625
- w_value: bfloat16 [1536, 1536], P('wshard'), may hold values from -0.15625 to 0.15625
- w_ogate: bfloat16 [1536, 1536], P('wshard'), may hold values from -0.15625 to 0.15625
- w_forget: bfloat16 [1536, 24], P('wshard'), may hold values from -0.15625 to 0.15625
- forget_bias: float32 [24], replicated, may hold values from 3.5 to 8
- w_out: bfloat16 [1536, 1536], P('wshard'), may hold values from -1 to 1
- norm_ffn: float32 [1536], replicated, may hold values from 0.1 to 1.9
- w_gate: bfloat16 [1536, 4096], P('wshard'), may hold values from -0.15625 to 0.15625
- w_up: bfloat16 [1536, 4096], P('wshard'), may hold values from -0.15625 to 0.15625
- w_down: bfloat16 [4096, 1536], P('wshard'), may hold values from -0.09375 to 0.09375
- output_grad: bfloat16 [8, 1024, 1536], P('wshard', 'seq'), may hold values from -6 to 6
Outputs:
- layer_output: bfloat16 [8, 1024, 1536], P('wshard', 'seq')
- grad_input: float32 [8, 1024, 1536], P('wshard', 'seq')
- grad_norm_attn: float32 [1536], replicated
- grad_w_query: float32 [1536, 1536], P('wshard')
- grad_w_key: float32 [1536, 1536], P('wshard')
- grad_w_value: float32 [1536, 1536], P('wshard')
- grad_w_ogate: float32 [1536, 1536], P('wshard')
- grad_w_forget: float32 [1536, 24], P('wshard')
- grad_forget_bias: float32 [24], replicated
- grad_w_out: float32 [1536, 1536], P('wshard')
- grad_norm_ffn: float32 [1536], replicated
- grad_w_gate: float32 [1536, 4096], P('wshard')
- grad_w_up: float32 [1536, 4096], P('wshard')
- grad_w_down: float32 [4096, 1536], P('wshard')
Inputs may be any that keep to these rules, and one draw needn't show every extreme that they name: Each sequence has 1024 slots of which the first lengths[s] are valid; in every draw one sequence is full and one has exactly 256 valid slots.
All inputs are finite; a program needn't handle non-finite values.
Results may differ from a plain program's by a relative error of at most 0.014.
Values may be sent and summed in bfloat16 or wider, within the bound.
A program may use at most 320 MiB of HBM per device.

v0:
```python
import jax
import jax.numpy as jnp
from jax import lax
from jax.sharding import PartitionSpec as P

EPS = 1e-06
NEG_FILL = -1e30
BF16 = jnp.bfloat16
F32 = jnp.float32


def product(left, right):
    return jnp.dot(left, right, preferred_element_type=F32)


def product_tn(left, right):
    return lax.dot_general(left, right, (((0,), (0,)), ((), ())), preferred_element_type=F32)


def product_nt(left, right):
    return lax.dot_general(left, right, (((1,), (1,)), ((), ())), preferred_element_type=F32)


def rms_norm(values, gain):
    return values * lax.rsqrt(jnp.mean(values * values, axis=-1, keepdims=True) + EPS) * gain


def gate_product(attended, gate_pre):
    return attended * jax.nn.sigmoid(gate_pre)


def swiglu(gate, upward):
    return jax.nn.silu(gate) * upward


def gather_rows(shard):
    return lax.all_gather(shard, "wshard", axis=0, tiled=True)


def scatter_rows(partial):
    return lax.psum_scatter(partial.astype(BF16), "wshard", scatter_dimension=0, tiled=True)


def gather_slots(shard):
    return lax.all_gather(shard, "seq", axis=0, tiled=True)


def scatter_slots(partial):
    return lax.psum_scatter(partial.astype(BF16), "seq", scatter_dimension=0, tiled=True).astype(
        F32
    )


def share_columns(share):
    return lax.all_gather(share, "seq", axis=1, tiled=True).astype(F32)


def block_scores(query_block, key_block, cum_rows, cum_keys, first_row, length, scale):
    plain = jnp.einsum("qhd,khd->hqk", query_block, key_block, preferred_element_type=F32) * scale
    plain = plain + cum_rows.T[:, :, None] - cum_keys.T[:, None, :]
    rows = first_row + jnp.arange(query_block.shape[0], dtype=jnp.int32)
    columns = jnp.arange(key_block.shape[0], dtype=jnp.int32)
    allowed = (columns[None, :] <= rows[:, None]) & (columns[None, :] < length)
    return jnp.where(allowed[None], plain, NEG_FILL)


def attention_forward(query, key, value, cumulative, length, scale, block):
    slots = query.shape[0]
    blocks = []
    log_totals = []
    for first in range(0, slots, block):
        last = first + block
        masked = block_scores(
            query[first:last],
            key[:last],
            cumulative[first:last],
            cumulative[:last],
            first,
            length,
            scale,
        )
        log_total = jax.nn.logsumexp(masked, axis=-1, keepdims=True)
        probability = jnp.exp(masked - log_total).astype(BF16)
        blocks.append(
            jnp.einsum("hqk,khd->qhd", probability, value[:last], preferred_element_type=F32)
        )
        log_totals.append(log_total)
    return (jnp.concatenate(blocks, axis=0).astype(BF16), log_totals)


def attention_backward(query, key, value, grad, cumulative, log_totals, length, scale, block):
    slots, heads, size = query.shape
    grad_query = []
    grad_key = jnp.zeros((slots, heads, size), F32)
    grad_value = jnp.zeros((slots, heads, size), F32)
    grad_cum = jnp.zeros((slots, heads), F32)
    for number, first in enumerate(range(0, slots, block)):
        last = first + block
        masked = block_scores(
            query[first:last],
            key[:last],
            cumulative[first:last],
            cumulative[:last],
            first,
            length,
            scale,
        )
        probability = jnp.exp(masked - log_totals[number])
        probability_low = probability.astype(BF16)
        grad_block = grad[first:last]
        grad_probability = jnp.einsum(
            "qhd,khd->hqk", grad_block, value[:last], preferred_element_type=F32
        )
        row_dot = jnp.sum(grad_probability * probability, axis=-1, keepdims=True)
        score_terms = probability * (grad_probability - row_dot)
        grad_scores = score_terms.astype(BF16)
        grad_cum = grad_cum.at[first:last].add(jnp.sum(score_terms, axis=2).T)
        grad_cum = grad_cum.at[:last].add(-jnp.sum(score_terms, axis=1).T)
        grad_query.append(
            jnp.einsum("hqk,khd->qhd", grad_scores, key[:last], preferred_element_type=F32)
        )
        grad_key = grad_key.at[:last].add(
            jnp.einsum("hqk,qhd->khd", grad_scores, query[first:last], preferred_element_type=F32)
        )
        grad_value = grad_value.at[:last].add(
            jnp.einsum("hqk,qhd->khd", probability_low, grad_block, preferred_element_type=F32)
        )
    grad_query = (jnp.concatenate(grad_query, axis=0) * scale).astype(BF16)
    return (grad_query, (grad_key * scale).astype(BF16), grad_value.astype(BF16), grad_cum)


def on_device(
    layer_input,
    lengths,
    norm_attn,
    w_query,
    w_key,
    w_value,
    w_ogate,
    w_forget,
    forget_bias,
    w_out,
    norm_ffn,
    w_gate,
    w_up,
    w_down,
    output_grad,
):
    tokens, width = layer_input.shape[1:]
    heads = forget_bias.shape[0]
    groups = lax.axis_size("seq")
    owners = lax.axis_size("wshard")
    local_heads = heads // groups
    head_size = width // heads
    slots = tokens * groups
    part = width // groups
    units = w_gate.shape[1]
    own_units = units // owners
    piece = own_units // groups
    local_units = units // groups
    block = min(512, slots)
    scale = head_size ** (-0.5)
    length = lengths[0]
    rank = lax.axis_index("seq")
    positions = rank * tokens + jnp.arange(tokens, dtype=jnp.int32)
    valid_slots = (positions < length).astype(F32)[:, None]
    inputs = layer_input[0].astype(F32)
    cotangent = output_grad[0].astype(F32) * valid_slots

    def columns(weight):
        return lax.dynamic_slice_in_dim(weight, rank * part, part, 1)

    def unit_columns(weight):
        cut = lax.dynamic_index_in_dim(
            weight.reshape(-1, owners, groups, piece), rank, 2, keepdims=False
        )
        return cut.reshape(-1, local_units)

    pad = -local_heads % 128
    forget_columns = jnp.pad(
        lax.dynamic_slice_in_dim(w_forget, rank * local_heads, local_heads, 1), ((0, 0), (0, pad))
    )
    normed_attn = gather_slots(rms_norm(inputs, norm_attn).astype(BF16))
    full_attn = gather_rows(
        jnp.concatenate(
            [columns(w_query), columns(w_key), columns(w_value), columns(w_ogate), forget_columns],
            axis=1,
        )
    )
    cut_out = gather_rows(columns(w_out))
    full_out = lax.all_to_all(cut_out, "seq", split_axis=0, concat_axis=1, tiled=True)
    full_gate_up = gather_rows(jnp.concatenate([unit_columns(w_gate), unit_columns(w_up)], axis=1))
    full_down = gather_rows(lax.dynamic_slice_in_dim(w_down, rank * piece, piece, 0))
    cotangent_low = gather_slots(cotangent.astype(BF16))
    query = product(normed_attn, full_attn[:, :part]).astype(BF16)
    key = product(normed_attn, full_attn[:, part : 2 * part]).astype(BF16)
    value = product(normed_attn, full_attn[:, 2 * part : 3 * part]).astype(BF16)
    gate_pre = product(normed_attn, full_attn[:, 3 * part : 4 * part])
    forget_pre = product(normed_attn, full_attn[:, 4 * part :])[:, :local_heads].astype(BF16)
    query = query.reshape(slots, local_heads, head_size)
    key = key.reshape(slots, local_heads, head_size)
    value = value.reshape(slots, local_heads, head_size)
    bias_local = lax.dynamic_slice_in_dim(forget_bias, rank * local_heads, local_heads)
    forget_total = forget_pre.astype(F32) + bias_local
    log_forget, pull_forget = jax.vjp(jax.nn.log_sigmoid, forget_total)
    cumulative = jnp.cumsum(log_forget, axis=0)
    head_output, log_totals = attention_forward(query, key, value, cumulative, length, scale, block)
    attended = head_output.reshape(slots, part).astype(F32)
    gated_full, pull_gate = jax.vjp(gate_product, attended, gate_pre)
    gated = gated_full.astype(BF16)
    middle = inputs + scatter_slots(product(gated, full_out))
    normed_ffn_full, pull_ffn_norm = jax.vjp(rms_norm, middle, norm_ffn)
    normed_ffn = gather_slots(normed_ffn_full.astype(BF16))
    gate_value = product(normed_ffn, full_gate_up[:, :local_units])
    up_value = product(normed_ffn, full_gate_up[:, local_units:])
    hidden_full, pull_swiglu = jax.vjp(swiglu, gate_value, up_value)
    hidden = hidden_full.astype(BF16)
    result = middle + scatter_slots(product(hidden, full_down))
    layer_output = result.astype(BF16)[None]
    grad_hidden = product_nt(cotangent_low, full_down)
    grad_gate_full, grad_up_full = pull_swiglu(grad_hidden)
    grad_gate_up = jnp.concatenate([grad_gate_full.astype(BF16), grad_up_full.astype(BF16)], axis=1)
    grad_normed_ffn = scatter_slots(product_nt(grad_gate_up, full_gate_up))
    share_down = scatter_rows(product_tn(hidden, cotangent_low))
    share_gate_up = scatter_rows(product_tn(normed_ffn, grad_gate_up))
    grad_middle_part, grad_norm_ffn = pull_ffn_norm(grad_normed_ffn)
    grad_middle = cotangent + grad_middle_part
    grad_branch = gather_slots(grad_middle.astype(BF16))
    grad_gated = product_nt(grad_branch, full_out)
    grad_w_out = product_tn(gated, grad_branch).astype(BF16)
    share_out = scatter_rows(
        lax.all_to_all(grad_w_out, "seq", split_axis=1, concat_axis=0, tiled=True)
    )
    grad_attended_full, grad_gate_pre_full = pull_gate(grad_gated)
    grad_attended = grad_attended_full.astype(BF16).reshape(slots, local_heads, head_size)
    grad_gate_pre = grad_gate_pre_full.astype(BF16)
    grad_query, grad_key, grad_value, grad_cum = attention_backward(
        query, key, value, grad_attended, cumulative, log_totals, length, scale, block
    )
    grad_log_forget = jnp.flip(jnp.cumsum(jnp.flip(grad_cum, 0), axis=0), 0)
    grad_forget_total = pull_forget(grad_log_forget)[0]
    grad_bias_local = jnp.sum(grad_forget_total, axis=0)
    grad_bias = lax.dynamic_update_slice_in_dim(
        jnp.zeros((heads,), F32), grad_bias_local, rank * local_heads, 0
    )
    grad_attn = jnp.concatenate(
        [
            grad_query.reshape(slots, part),
            grad_key.reshape(slots, part),
            grad_value.reshape(slots, part),
            grad_gate_pre,
            jnp.pad(grad_forget_total.astype(BF16), ((0, 0), (0, pad))),
        ],
        axis=1,
    )
    grad_normed_attn = scatter_slots(product_nt(grad_attn, full_attn))
    share_attn = scatter_rows(product_tn(normed_attn, grad_attn))
    unused_normed, pull_attn_norm = jax.vjp(rms_norm, inputs, norm_attn)
    grad_input_part, grad_norm_attn = pull_attn_norm(grad_normed_attn)
    grad_input = (grad_middle + grad_input_part)[None]
    rows = w_query.shape[0]
    all_down = lax.all_gather(share_down, "seq", axis=0, tiled=True).astype(F32)
    all_gate_up = lax.all_gather(share_gate_up, "seq", axis=0, tiled=False)
    all_gate_up = all_gate_up.reshape(groups, rows, 2, owners, piece).transpose(2, 1, 3, 0, 4)
    all_gate_up = all_gate_up.reshape(2, rows, units).astype(F32)
    all_out = share_columns(share_out)
    all_attn = lax.all_gather(share_attn, "seq", axis=0, tiled=False)

    def whole(first, size):
        cut = all_attn[:, :, first : first + size].transpose(1, 0, 2)
        return cut.reshape(rows, groups * size).astype(F32)

    small = lax.psum((grad_norm_attn, grad_norm_ffn, grad_bias), ("seq", "wshard"))
    return (
        layer_output,
        grad_input,
        small[0],
        whole(0, part),
        whole(part, part),
        whole(2 * part, part),
        whole(3 * part, part),
        whole(4 * part, local_heads),
        small[2],
        all_out,
        small[1],
        all_gate_up[0],
        all_gate_up[1],
        all_down,
    )


def solution(mesh):
    rows = P("wshard", None)
    slots = P("wshard", "seq", None)
    return jax.shard_map(
        on_device,
        mesh=mesh,
        in_specs=(
            slots,
            P("wshard"),
            P(),
            rows,
            rows,
            rows,
            rows,
            rows,
            P(),
            rows,
            P(),
            rows,
            rows,
            rows,
            slots,
        ),
        out_specs=(
            slots,
            slots,
            P(),
            rows,
            rows,
            rows,
            rows,
            rows,
            P(),
            rows,
            P(),
            rows,
            rows,
            rows,
        ),
        check_vma=False,
    )
```

profile of v0, /device:TPU:0, one launch (start us, length us, event | category | flops | bytes accessed | tf_op | source)
XLA Modules:
  0.0 979.0 jit_solution(494081339802589565)
XLA Ops:
  19.4 16.4 %all-gather.18.cloned.1.call-done = bf16[1536,384]{1,0:T(8,128)(2,1)} async-done(((bf16[192,384]{1,0:T(8,128)(2,1)}), bf16[1536,384]{1,0:T(8,128)(2,1)}) %all-gather.18.cloned.1.call-update) | async-done | bytes 1179664 | tf_op jit(solution)/shard_map/all_gather | solution.py:37
  41.4 21.1 %all-to-all-done = bf16[4,384,384]{2,1,0:T(8,128)(2,1)S(1)} async-done(((bf16[4,384,384]{2,1,0:T(8,128)(2,1)}), bf16[4,384,384]{2,1,0:T(8,128)(2,1)S(1)}, u32[]{:S(2)}, u32[]{:S(2)}) %all-to-all-start) | async-done | bytes 1179680 | tf_op jit(solution)/shard_map/all_to_all | solution.py:191
  64.0 23.1 %all-gather.14.cloned.1.call-done = bf16[1024,1536]{1,0:T(8,128)(2,1)} async-done(((bf16[256,1536]{1,0:T(8,128)(2,1)}), bf16[1024,1536]{1,0:T(8,128)(2,1)}) %all-gather.14.cloned.1.call-update) | async-done | bytes 3145744 | tf_op jit(solution)/shard_map/all_gather | solution.py:45
  87.0 57.1 %all-gather.16.cloned.1.call-done = bf16[1536,1664]{1,0:T(8,128)(2,1)} async-done(((bf16[192,1664]{1,0:T(8,128)(2,1)}), bf16[1536,1664]{1,0:T(8,128)(2,1)}) %all-gather.16.cloned.1.call-update) | async-done | bytes 5111824 | tf_op jit(solution)/shard_map/all_gather | solution.py:37
  199.1 25.4 %reduce-scatter.9.cloned.1.call-done = bf16[256,1536]{1,0:T(8,128)(2,1)} async-done(((bf16[1024,1536]{1,0:T(8,128)(2,1)}), bf16[256,1536]{1,0:T(8,128)(2,1)}) %reduce-scatter.9.cloned.1.call-update) | async-done | bytes 786448 | tf_op jit(solution)/shard_map/reduce_scatter | solution.py:49
  228.6 42.0 %all-gather.26.cloned.1.call-done = bf16[1024,1536]{1,0:T(8,128)(2,1)} async-done(((bf16[256,1536]{1,0:T(8,128)(2,1)}), bf16[1024,1536]{1,0:T(8,128)(2,1)}) %all-gather.26.cloned.1.call-update) | async-done | bytes 3145744 | tf_op jit(solution)/shard_map/all_gather | solution.py:45
  270.7 40.3 %all-gather.24.cloned.1.call-done = bf16[1024,1536]{1,0:T(8,128)(2,1)} async-done(((bf16[128,1536]{1,0:T(8,128)(2,1)}), bf16[1024,1536]{1,0:T(8,128)(2,1)}) %all-gather.24.cloned.1.call-update) | async-done | bytes 3145744 | tf_op jit(solution)/shard_map/all_gather | solution.py:37
  319.2 57.6 %all-gather.22.cloned.1.call-done = bf16[1536,2048]{1,0:T(8,128)(2,1)} async-done(((bf16[192,2048]{1,0:T(8,128)(2,1)}), bf16[1536,2048]{1,0:T(8,128)(2,1)}) %all-gather.22.cloned.1.call-update) | async-done | bytes 6291472 | tf_op jit(solution)/shard_map/all_gather | solution.py:37
  376.8 44.9 %all-gather.20.cloned.1.call-done = bf16[1024,1536]{1,0:T(8,128)(2,1)} async-done(((bf16[256,1536]{1,0:T(8,128)(2,1)}), bf16[1024,1536]{1,0:T(8,128)(2,1)}) %all-gather.20.cloned.1.call-update) | async-done | bytes 3145744 | tf_op jit(solution)/shard_map/all_gather | solution.py:45
  440.1 9.4 convolution_convert_fusion.2
  450.0 43.6 %reduce-scatter.13.cloned.1.call-done = bf16[256,1536]{1,0:T(8,128)(2,1)} async-done(((bf16[1024,1536]{1,0:T(8,128)(2,1)}), bf16[256,1536]{1,0:T(8,128)(2,1)}) %reduce-scatter.13.cloned.1.call-update) | async-done | bytes 786448 | tf_op jit(solution)/shard_map/reduce_scatter | solution.py:49
  506.5 11.6 %convolution_convert_fusion.1 = bf16[1536,2048]{1,0:T(8,128)(2,1)} fusion(bf16[1024,1536]{1,0:T(8,128)(2,1)} %all-gather.20.cloned.1.call-done, bf16[1024,1024]{0,1:T(8,128)(2,1)} %get-tuple-element.150, bf16[1024,1024]{0,1:T(8,128)(2,1)} %copy-done.58), kind=kOutput, calls=%fused_computation.7 | convolution fusion | flops 6453985280 | bytes 13631488 | tf_op jit(solution)/shard_map/dot_general | solution.py:17
  518.2 24.6 %all-gather.28.cloned.1.call-done = bf16[1024,1536]{1,0:T(8,128)(2,1)} async-done(((bf16[256,1536]{1,0:T(8,128)(2,1)}), bf16[1024,1536]{1,0:T(8,128)(2,1)}) %all-gather.28.cloned.1.call-update) | async-done | bytes 3145744 | tf_op jit(solution)/shard_map/all_gather | solution.py:45
  607.3 18.7 %all_to_all.38 = bf16[384,4,384]{2,0,1:T(8,128)(2,1)} all-to-all(bf16[384,4,384]{2,0,1:T(8,128)(2,1)S(1)} %bitcast.215), channel_id=1, replica_groups=mesh['seq'=4,'wshard'=8] {'seq'}, dimensions={1} | all-to-all | bytes 2359296 | tf_op jit(solution)/shard_map/all_to_all | solution.py:232
  626.0 31.2 %reduce-scatter.21.cloned.1.call-done = bf16[192,2048]{1,0:T(8,128)(2,1)} async-done(((bf16[1536,2048]{1,0:T(8,128)(2,1)}), bf16[192,2048]{1,0:T(8,128)(2,1)}) %reduce-scatter.21.cloned.1.call-update) | async-done | bytes 786448 | tf_op jit(solution)/shard_map/reduce_scatter | solution.py:41
  657.3 10.2 %convolution_convert_fusion.3 = bf16[1024,1536]{1,0:T(8,128)(2,1)} fusion(bf16[1024,1664]{0,1:T(8,128)(2,1)} %copy-done.36, bf16[1536,1664]{1,0:T(8,128)(2,1)} %all-gather.16.cloned.1.call-done), kind=kOutput, calls=%fused_computation.25 | convolution fusion | flops 5236064256 | bytes 11665408 | tf_op jit(solution)/shard_map/dot_general | solution.py:21
  675.3 41.0 %reduce-scatter.17.cloned.1.call-done = bf16[192,1664]{1,0:T(8,128)(2,1)} async-done(((bf16[1536,1664]{1,0:T(8,128)(2,1)}), bf16[192,1664]{1,0:T(8,128)(2,1)}) %reduce-scatter.17.cloned.1.call-update) | async-done | bytes 638992 | tf_op jit(solution)/shard_map/reduce_scatter | solution.py:41
  716.3 31.0 %all-gather.30.cloned.1.call-done = bf16[512,1536]{1,0:T(8,128)(2,1)} async-done(((bf16[128,1536]{1,0:T(8,128)(2,1)}), bf16[512,1536]{1,0:T(8,128)(2,1)}) %all-gather.30.cloned.1.call-update) | async-done | bytes 1572880 | tf_op jit(solution)/shard_map/all_gather | solution.py:262
  750.9 31.5 %reduce-scatter.19.cloned.1.call-done = bf16[192,384]{1,0:T(8,128)(2,1)} async-done(((bf16[1536,384]{1,0:T(8,128)(2,1)}), bf16[192,384]{1,0:T(8,128)(2,1)}) %reduce-scatter.19.cloned.1.call-update) | async-done | bytes 147472 | tf_op jit(solution)/shard_map/reduce_scatter | solution.py:41
  782.5 14.6 %all_gather.52 = bf16[192,1536]{1,0:T(8,128)(2,1)S(1)} all-gather(bf16[192,384]{1,0:T(8,128)(2,1)} %reduce-scatter.19.cloned.1.call-done), channel_id=1, replica_groups=mesh['seq'=4,'wshard'=8] {'seq'}, dimensions={1}, use_global_device_ids=true | all-gather | bytes 737280 | tf_op jit(solution)/shard_map/all_gather | solution.py:55
  798.3 28.1 %all-gather.34.cloned.1.call-done = bf16[768,2048]{1,0:T(8,128)(2,1)} async-done(((bf16[192,2048]{1,0:T(8,128)(2,1)}), bf16[768,2048]{1,0:T(8,128)(2,1)}) %all-gather.34.cloned.1.call-update) | async-done | bytes 3145744 | tf_op jit(solution)/shard_map/all_gather | solution.py:263
  852.5 20.6 %reduce-scatter.15.cloned.1.call-done = bf16[256,1536]{1,0:T(8,128)(2,1)} async-done(((bf16[1024,1536]{1,0:T(8,128)(2,1)}), bf16[256,1536]{1,0:T(8,128)(2,1)}) %reduce-scatter.15.cloned.1.call-update) | async-done | bytes 786448 | tf_op jit(solution)/shard_map/reduce_scatter | solution.py:49
  875.0 40.3 %all-reduce.5 = (f32[1536]{0:T(1024)}, f32[24]{0:T(128)}, f32[1536]{0:T(1024)}) all-reduce(f32[1536]{0:T(1024)S(1)} %get-tuple-element.140, f32[24]{0:T(128)S(1)} %negate_dynamic-update-slice_fusion, f32[1536]{0:T(1024)S(1)} %copy-done.41), channel_id=1, replica_groups=mesh['seq'=4,'wshard'=8] {'seq','wshard'}, use_global_device_ids=true, to_apply=%region_23.24 | all-reduce | flops 3096 | bytes 24768 | tf_op jit(solution)/shard_map/psum | solution.py:273
  924.7 36.9 %all-gather.32.cloned.1.call-done = bf16[768,1664]{1,0:T(8,128)(2,1)} async-done(((bf16[192,1664]{1,0:T(8,128)(2,1)}), bf16[768,1664]{1,0:T(8,128)(2,1)}) %all-gather.32.cloned.1.call-update) | async-done | bytes 2555920 | tf_op jit(solution)/shard_map/all_gather | solution.py:267
  (305 shorter events, 241.3 us)
Async XLA Ops:
  7.2 176.7 %copy-start = (bf16[512,1536]{1,0:T(8,128)(2,1)S(1)}, bf16[512,1536]{1,0:T(8,128)(2,1)}, u32[]{:S(2)}) copy-start(bf16[512,1536]{1,0:T(8,128)(2,1)} %param.50) | copy-start | bytes 4718596
  7.2 28.6 %all-gather.18.cloned.1.call-start = ((), (), s32[]{:S(2)}) async-start(), calls=%async_computation.12 | async-start | bytes 1327104 | tf_op jit(solution)/shard_map/all_gather | solution.py:37
  9.0 78.1 %all-gather.14.cloned.1.call-start = ((), (), s32[]{:S(2)}) async-start(), calls=%async_computation.10 | async-start | bytes 3932160 | tf_op jit(solution)/shard_map/all_gather | solution.py:45
  13.8 130.4 %all-gather.16.cloned.1.call-start = ((), (), s32[]{:S(2)}) async-start(), calls=%async_computation.11 | async-start | bytes 5750784 | tf_op jit(solution)/shard_map/all_gather | solution.py:37
  35.8 26.8 %all-to-all-start = ((bf16[4,384,384]{2,1,0:T(8,128)(2,1)}), bf16[4,384,384]{2,1,0:T(8,128)(2,1)S(1)}, u32[]{:S(2)}, u32[]{:S(2)}) async-start(bf16[4,384,384]{2,1,0:T(8,128)(2,1)} %bitcast.248), calls=%async_computation | async-start | bytes 2359296 | tf_op jit(solution)/shard_map/all_to_all | solution.py:191
  39.3 185.2 %reduce-scatter.9.cloned.1.call-start = ((), (), s32[]{:S(2)}) async-start(), calls=%async_computation.13 | async-start | bytes 3932160 | tf_op jit(solution)/shard_map/reduce_scatter | solution.py:49
  40.1 107.2 %copy-start.52 = (f32[6]{0:T(128)}, f32[6]{0:T(128)S(1)}, u32[]{:S(2)}) copy-start(f32[6]{0:T(128)S(1)} %dynamic_slice.36) | copy-start | bytes 76
  181.7 89.0 %all-gather.26.cloned.1.call-start = ((), (), s32[]{:S(2)}) async-start(), calls=%async_computation.18 | async-start | bytes 3932160 | tf_op jit(solution)/shard_map/all_gather | solution.py:45
  182.8 313.2 %copy-start.46 = (f32[256]{0:T(256)}, f32[256]{0:T(256)S(1)}, u32[]{:S(2)}) copy-start(f32[256]{0:T(256)S(1)} %compare_convert_fusion) | copy-start | bytes 3076
  183.9 127.1 %all-gather.24.cloned.1.call-start = ((), (), s32[]{:S(2)}) async-start(), calls=%async_computation.16 | async-start | bytes 3538944 | tf_op jit(solution)/shard_map/all_gather | solution.py:37
  184.7 192.1 %all-gather.22.cloned.1.call-start = ((), (), s32[]{:S(2)}) async-start(), calls=%async_computation.15 | async-start | bytes 7077888 | tf_op jit(solution)/shard_map/all_gather | solution.py:37
  199.0 222.7 %all-gather.20.cloned.1.call-start = ((), (), s32[]{:S(2)}) async-start(), calls=%async_computation.14 | async-start | bytes 3932160 | tf_op jit(solution)/shard_map/all_gather | solution.py:45
  226.0 270.0 %copy-start.42 = (f32[256]{0:T(256)}, f32[256]{0:T(256)S(1)}, u32[]{:S(2)}) copy-start(f32[256]{0:T(256)S(1)} %fusion.73) | copy-start | bytes 3076
  228.4 265.2 %reduce-scatter.13.cloned.1.call-start = ((), (), s32[]{:S(2)}) async-start(), calls=%async_computation.19 | async-start | bytes 3932160 | tf_op jit(solution)/shard_map/reduce_scatter | solution.py:49
  449.5 93.2 %all-gather.28.cloned.1.call-start = ((), (), s32[]{:S(2)}) async-start(), calls=%async_computation.20 | async-start | bytes 3932160 | tf_op jit(solution)/shard_map/all_gather | solution.py:45
  498.7 104.0 %reduce-scatter.23.cloned.1.call-start = ((), (), s32[]{:S(2)}) async-start(), calls=%async_computation.25 | async-start | bytes 3538944 | tf_op jit(solution)/shard_map/reduce_scatter | solution.py:41
  506.4 150.8 %reduce-scatter.21.cloned.1.call-start = ((), (), s32[]{:S(2)}) async-start(), calls=%async_computation.24 | async-start | bytes 7077888 | tf_op jit(solution)/shard_map/reduce_scatter | solution.py:41
  518.1 198.2 %reduce-scatter.17.cloned.1.call-start = ((), (), s32[]{:S(2)}) async-start(), calls=%async_computation.22 | async-start | bytes 5750784 | tf_op jit(solution)/shard_map/reduce_scatter | solution.py:41
  602.7 144.7 %all-gather.30.cloned.1.call-start = ((), (), s32[]{:S(2)}) async-start(), calls=%async_computation.26 | async-start | bytes 1966080 | tf_op jit(solution)/shard_map/all_gather | solution.py:262
  603.3 179.2 %reduce-scatter.19.cloned.1.call-start = ((), (), s32[]{:S(2)}) async-start(), calls=%async_computation.23 | async-start | bytes 1327104 | tf_op jit(solution)/shard_map/reduce_scatter | solution.py:41
  626.0 200.4 %all-gather.34.cloned.1.call-start = ((), (), s32[]{:S(2)}) async-start(), calls=%async_computation.28 | async-start | bytes 3932160 | tf_op jit(solution)/shard_map/all_gather | solution.py:263
  657.3 215.9 %reduce-scatter.15.cloned.1.call-start = ((), (), s32[]{:S(2)}) async-start(), calls=%async_computation.21 | async-start | bytes 3932160 | tf_op jit(solution)/shard_map/reduce_scatter | solution.py:49
  667.5 253.2 %reduce-scatter.11.cloned.1.call-start = ((), (), s32[]{:S(2)}) async-start(), calls=%async_computation.17 | async-start | bytes 3932160 | tf_op jit(solution)/shard_map/reduce_scatter | solution.py:49
  675.3 286.3 %all-gather.32.cloned.1.call-start = ((), (), s32[]{:S(2)}) async-start(), calls=%async_computation.27 | async-start | bytes 3194880 | tf_op jit(solution)/shard_map/all_gather | solution.py:267
  (65 other events, 886.0 us)
Sparse Core Ops, SparseCore 0:
  10.2 25.4 all-gather.17
  38.2 48.8 all-gather.13
  89.3 54.8 all-gather.15
  181.8 42.6 reduce-scatter.8
  226.8 43.8 all-gather.25
  272.7 38.2 all-gather.23
  313.2 63.5 all-gather.21
  379.2 42.4 all-gather.19
  449.6 43.8 reduce-scatter.12
  498.9 43.8 all-gather.27
  545.6 40.3 reduce-scatter.22
  588.2 69.0 reduce-scatter.20
  659.6 56.7 reduce-scatter.16
  718.0 29.3 all-gather.29
  749.5 32.9 reduce-scatter.18
  784.2 42.1 all-gather.33
  829.2 43.8 reduce-scatter.14
  876.0 44.6 reduce-scatter.10
  922.6 38.9 all-gather.31
where the time goes:
time: 989 us; the launch traced here: 979 us
  waiting for transfers between devices  623 us (63%)
  matrix products  140 us (14%)
  blocking collectives  73.7 us (7%)
  local copies, waits for them, and re-layouts  68.5 us (7%)
  other arithmetic  53.1 us (5%)
  between operations  16.2 us (2%)
    all_gather x4, waiting for transfers between devices, gather_rows(): return lax.all_gather(shard, 'wshard', axis=0, tiled=True)  171 us
    all_gather x4, waiting for transfers between devices, gather_slots(): return lax.all_gather(shard, 'seq', axis=0, tiled=True)  135 us
    reduce_scatter x4, waiting for transfers between devices, scatter_rows(): lax.psum_scatter(partial.astype(BF16), 'wshard', scatter_dimension=0, til...  104 us
    reduce_scatter x4, waiting for transfers between devices, scatter_slots(): lax.psum_scatter(partial.astype(BF16), 'seq', scatter_dimension=0, tiled=...  95.1 us
    dot_general x9, matrix products, product(): return jnp.dot(left, right, preferred_element_type=F32)  44.1 us
    psum x1, blocking collectives, on_device(): lax.psum((grad_norm_attn, grad_norm_ffn, grad_bias), ('seq', 'wshard'))  40.3 us
    all_gather x1, waiting for transfers between devices, on_device(): all_attn = lax.all_gather(share_attn, 'seq', axis=0, tiled=False)  36.9 us
    dot_general x4, matrix products, product_nt(): lax.dot_general(left, right, (((1,), (1,)), ((), ())), preferred_element_...  33.1 us
  transfers between devices with their start and end apart: 20, of which 19 were waited for; matrix products, arithmetic and copies ran while one was open for 18% of the time, Pallas kernels for 0%

commit v1 on v0

--- a/solution.py
+++ b/solution.py
@@ -188,7 +188,10 @@
         )
     )
     cut_out = gather_rows(columns(w_out))
-    full_out = lax.all_to_all(cut_out, "seq", split_axis=0, concat_axis=1, tiled=True)
+    full_out = jnp.concatenate(
+        lax.all_to_all(jnp.stack(jnp.split(cut_out, lax.axis_size("seq"), axis=0)), "seq", 0, 0),
+        axis=1,
+    )
     full_gate_up = gather_rows(jnp.concatenate([unit_columns(w_gate), unit_columns(w_up)], axis=1))
     full_down = gather_rows(lax.dynamic_slice_in_dim(w_down, rank * piece, piece, 0))
     cotangent_low = gather_slots(cotangent.astype(BF16))

time: 989 us -> 989 us (level)
    all_gather x4, waiting for transfers between devices: 135 us -> 159 us  [gather_slots(): return lax.all_gather(shard, 'seq', axis=0, tiled=True)]
    all_to_all x1, waiting for transfers between devices: 21.1 us -> 0.01 us  [on_device(): lax.all_to_all(jnp.stack(jnp.split(cut_out, lax.axis_size('seq'), axis=0)...]
  transfers between devices with their start and end apart: 20 -> 20, of which waited for: 19 -> 18; matrix products, arithmetic and copies ran while one was open for 18% -> 21% of each run, Pallas kernels for 0% -> 0%
where the time goes in v1:
time: 989 us; the launch traced here: 984 us
  waiting for transfers between devices  624 us (63%)
  matrix products  142 us (14%)
  blocking collectives  73.5 us (7%)
  local copies, waits for them, and re-layouts  67.6 us (7%)
  other arithmetic  54.6 us (6%)
  between operations  16 us (2%)
    all_gather x4, waiting for transfers between devices, gather_rows(): return lax.all_gather(shard, 'wshard', axis=0, tiled=True)  169 us
    all_gather x4, waiting for transfers between devices, gather_slots(): return lax.all_gather(shard, 'seq', axis=0, tiled=True)  159 us
    reduce_scatter x4, waiting for transfers between devices, scatter_rows(): lax.psum_scatter(partial.astype(BF16), 'wshard', scatter_dimension=0, til...  104 us
    reduce_scatter x4, waiting for transfers between devices, scatter_slots(): lax.psum_scatter(partial.astype(BF16), 'seq', scatter_dimension=0, tiled=...  95.3 us
    dot_general x9, matrix products, product(): return jnp.dot(left, right, preferred_element_type=F32)  45.8 us
    psum x1, blocking collectives, on_device(): lax.psum((grad_norm_attn, grad_norm_ffn, grad_bias), ('seq', 'wshard'))  40.3 us
    all_gather x1, waiting for transfers between devices, on_device(): all_attn = lax.all_gather(share_attn, 'seq', axis=0, tiled=False)  36.9 us
    dot_general x4, matrix products, product_nt(): lax.dot_general(left, right, (((1,), (1,)), ((), ())), preferred_element_...  33.1 us
  transfers between devices with their start and end apart: 20, of which 18 were waited for; matrix products, arithmetic and copies ran while one was open for 21% of the time, Pallas kernels for 0%

profile of v1, /device:TPU:0, one launch (start us, length us, event | category | flops | bytes accessed | tf_op | source)
XLA Modules:
  0.0 984.1 jit_solution(9195829652803567938)
XLA Ops:
  21.5 14.3 %all-gather.18.cloned.1.call-done = bf16[1536,384]{1,0:T(8,128)(2,1)} async-done(((bf16[192,384]{1,0:T(8,128)(2,1)}), bf16[1536,384]{1,0:T(8,128)(2,1)}) %all-gather.18.cloned.1.call-update) | async-done | bytes 1179664 | tf_op jit(solution)/shard_map/all_gather | solution.py:37
  43.5 47.5 %all-gather.14.cloned.1.call-done = bf16[1024,1536]{1,0:T(8,128)(2,1)} async-done(((bf16[256,1536]{1,0:T(8,128)(2,1)}), bf16[1024,1536]{1,0:T(8,128)(2,1)}) %all-gather.14.cloned.1.call-update) | async-done | bytes 3145744 | tf_op jit(solution)/shard_map/all_gather | solution.py:45
  91.1 57.1 %all-gather.16.cloned.1.call-done = bf16[1536,1664]{1,0:T(8,128)(2,1)} async-done(((bf16[192,1664]{1,0:T(8,128)(2,1)}), bf16[1536,1664]{1,0:T(8,128)(2,1)}) %all-gather.16.cloned.1.call-update) | async-done | bytes 5111824 | tf_op jit(solution)/shard_map/all_gather | solution.py:37
  204.1 25.4 %reduce-scatter.9.cloned.1.call-done = bf16[256,1536]{1,0:T(8,128)(2,1)} async-done(((bf16[1024,1536]{1,0:T(8,128)(2,1)}), bf16[256,1536]{1,0:T(8,128)(2,1)}) %reduce-scatter.9.cloned.1.call-update) | async-done | bytes 786448 | tf_op jit(solution)/shard_map/reduce_scatter | solution.py:49
  233.9 41.8 %all-gather.26.cloned.1.call-done = bf16[1024,1536]{1,0:T(8,128)(2,1)} async-done(((bf16[256,1536]{1,0:T(8,128)(2,1)}), bf16[1024,1536]{1,0:T(8,128)(2,1)}) %all-gather.26.cloned.1.call-update) | async-done | bytes 3145744 | tf_op jit(solution)/shard_map/all_gather | solution.py:45
  275.7 40.3 %all-gather.24.cloned.1.call-done = bf16[1024,1536]{1,0:T(8,128)(2,1)} async-done(((bf16[128,1536]{1,0:T(8,128)(2,1)}), bf16[1024,1536]{1,0:T(8,128)(2,1)}) %all-gather.24.cloned.1.call-update) | async-done | bytes 3145744 | tf_op jit(solution)/shard_map/all_gather | solution.py:37
  324.3 57.6 %all-gather.22.cloned.1.call-done = bf16[1536,2048]{1,0:T(8,128)(2,1)} async-done(((bf16[192,2048]{1,0:T(8,128)(2,1)}), bf16[1536,2048]{1,0:T(8,128)(2,1)}) %all-gather.22.cloned.1.call-update) | async-done | bytes 6291472 | tf_op jit(solution)/shard_map/all_gather | solution.py:37
  381.9 44.9 %all-gather.20.cloned.1.call-done = bf16[1024,1536]{1,0:T(8,128)(2,1)} async-done(((bf16[256,1536]{1,0:T(8,128)(2,1)}), bf16[1024,1536]{1,0:T(8,128)(2,1)}) %all-gather.20.cloned.1.call-update) | async-done | bytes 3145744 | tf_op jit(solution)/shard_map/all_gather | solution.py:45
  435.3 8.5 fusion.4
  445.1 9.4 convolution_convert_fusion.2
  454.7 43.8 %reduce-scatter.13.cloned.1.call-done = bf16[256,1536]{1,0:T(8,128)(2,1)} async-done(((bf16[1024,1536]{1,0:T(8,128)(2,1)}), bf16[256,1536]{1,0:T(8,128)(2,1)}) %reduce-scatter.13.cloned.1.call-update) | async-done | bytes 786448 | tf_op jit(solution)/shard_map/reduce_scatter | solution.py:49
  511.4 11.6 %convolution_convert_fusion.1 = bf16[1536,2048]{1,0:T(8,128)(2,1)} fusion(bf16[1024,1536]{1,0:T(8,128)(2,1)} %all-gather.20.cloned.1.call-done, bf16[1024,1024]{0,1:T(8,128)(2,1)} %get-tuple-element.150, bf16[1024,1024]{0,1:T(8,128)(2,1)} %copy-done.60), kind=kOutput, calls=%fused_computation.7 | convolution fusion | flops 6453985280 | bytes 13631488 | tf_op jit(solution)/shard_map/dot_general | solution.py:17
  523.1 24.6 %all-gather.28.cloned.1.call-done = bf16[1024,1536]{1,0:T(8,128)(2,1)} async-done(((bf16[256,1536]{1,0:T(8,128)(2,1)}), bf16[1024,1536]{1,0:T(8,128)(2,1)}) %all-gather.28.cloned.1.call-update) | async-done | bytes 3145744 | tf_op jit(solution)/shard_map/all_gather | solution.py:45
  612.5 18.7 %all_to_all.24 = bf16[384,4,384]{2,0,1:T(8,128)(2,1)} all-to-all(bf16[384,4,384]{2,0,1:T(8,128)(2,1)S(1)} %bitcast.218), channel_id=1, replica_groups=mesh['seq'=4,'wshard'=8] {'seq'}, dimensions={1} | all-to-all | bytes 2359296 | tf_op jit(solution)/shard_map/all_to_all | solution.py:235
  631.2 31.0 %reduce-scatter.21.cloned.1.call-done = bf16[192,2048]{1,0:T(8,128)(2,1)} async-done(((bf16[1536,2048]{1,0:T(8,128)(2,1)}), bf16[192,2048]{1,0:T(8,128)(2,1)}) %reduce-scatter.21.cloned.1.call-update) | async-done | bytes 786448 | tf_op jit(solution)/shard_map/reduce_scatter | solution.py:41
  662.3 10.1 %convolution_convert_fusion.3 = bf16[1024,1536]{1,0:T(8,128)(2,1)} fusion(bf16[1024,1664]{0,1:T(8,128)(2,1)} %copy-done.38, bf16[1536,1664]{1,0:T(8,128)(2,1)} %all-gather.16.cloned.1.call-done), kind=kOutput, calls=%fused_computation.25 | convolution fusion | flops 5236064256 | bytes 11665408 | tf_op jit(solution)/shard_map/dot_general | solution.py:21
  680.3 41.4 %reduce-scatter.17.cloned.1.call-done = bf16[192,1664]{1,0:T(8,128)(2,1)} async-done(((bf16[1536,1664]{1,0:T(8,128)(2,1)}), bf16[192,1664]{1,0:T(8,128)(2,1)}) %reduce-scatter.17.cloned.1.call-update) | async-done | bytes 638992 | tf_op jit(solution)/shard_map/reduce_scatter | solution.py:41
  721.7 31.0 %all-gather.30.cloned.1.call-done = bf16[512,1536]{1,0:T(8,128)(2,1)} async-done(((bf16[128,1536]{1,0:T(8,128)(2,1)}), bf16[512,1536]{1,0:T(8,128)(2,1)}) %all-gather.30.cloned.1.call-update) | async-done | bytes 1572880 | tf_op jit(solution)/shard_map/all_gather | solution.py:265
  756.3 31.5 %reduce-scatter.19.cloned.1.call-done = bf16[192,384]{1,0:T(8,128)(2,1)} async-done(((bf16[1536,384]{1,0:T(8,128)(2,1)}), bf16[192,384]{1,0:T(8,128)(2,1)}) %reduce-scatter.19.cloned.1.call-update) | async-done | bytes 147472 | tf_op jit(solution)/shard_map/reduce_scatter | solution.py:41
  787.8 14.5 %all_gather.52 = bf16[192,1536]{1,0:T(8,128)(2,1)S(1)} all-gather(bf16[192,384]{1,0:T(8,128)(2,1)} %reduce-scatter.19.cloned.1.call-done), channel_id=1, replica_groups=mesh['seq'=4,'wshard'=8] {'seq'}, dimensions={1}, use_global_device_ids=true | all-gather | bytes 737280 | tf_op jit(solution)/shard_map/all_gather | solution.py:55
  803.5 28.3 %all-gather.34.cloned.1.call-done = bf16[768,2048]{1,0:T(8,128)(2,1)} async-done(((bf16[192,2048]{1,0:T(8,128)(2,1)}), bf16[768,2048]{1,0:T(8,128)(2,1)}) %all-gather.34.cloned.1.call-update) | async-done | bytes 3145744 | tf_op jit(solution)/shard_map/all_gather | solution.py:266
  857.9 20.6 %reduce-scatter.15.cloned.1.call-done = bf16[256,1536]{1,0:T(8,128)(2,1)} async-done(((bf16[1024,1536]{1,0:T(8,128)(2,1)}), bf16[256,1536]{1,0:T(8,128)(2,1)}) %reduce-scatter.15.cloned.1.call-update) | async-done | bytes 786448 | tf_op jit(solution)/shard_map/reduce_scatter | solution.py:49
  880.4 40.3 %all-reduce.5 = (f32[1536]{0:T(1024)}, f32[24]{0:T(128)}, f32[1536]{0:T(1024)}) all-reduce(f32[1536]{0:T(1024)S(1)} %get-tuple-element.140, f32[24]{0:T(128)S(1)} %negate_dynamic-update-slice_fusion, f32[1536]{0:T(1024)S(1)} %copy-done.43), channel_id=1, replica_groups=mesh['seq'=4,'wshard'=8] {'seq','wshard'}, use_global_device_ids=true, to_apply=%region_23.24 | all-reduce | flops 3096 | bytes 24768 | tf_op jit(solution)/shard_map/psum | solution.py:276
  930.1 36.9 %all-gather.32.cloned.1.call-done = bf16[768,1664]{1,0:T(8,128)(2,1)} async-done(((bf16[192,1664]{1,0:T(8,128)(2,1)}), bf16[768,1664]{1,0:T(8,128)(2,1)}) %all-gather.32.cloned.1.call-update) | async-done | bytes 2555920 | tf_op jit(solution)/shard_map/all_gather | solution.py:270
  (314 shorter events, 236.7 us)
Async XLA Ops:
  7.2 181.8 %copy-start = (bf16[512,1536]{1,0:T(8,128)(2,1)S(1)}, bf16[512,1536]{1,0:T(8,128)(2,1)}, u32[]{:S(2)}) copy-start(bf16[512,1536]{1,0:T(8,128)(2,1)} %param.50) | copy-start | bytes 4718596
  7.2 28.6 %all-gather.18.cloned.1.call-start = ((), (), s32[]{:S(2)}) async-start(), calls=%async_computation.12 | async-start | bytes 1327104 | tf_op jit(solution)/shard_map/all_gather | solution.py:37
  9.0 82.1 %all-gather.14.cloned.1.call-start = ((), (), s32[]{:S(2)}) async-start(), calls=%async_computation.10 | async-start | bytes 3932160 | tf_op jit(solution)/shard_map/all_gather | solution.py:45
  13.8 134.4 %all-gather.16.cloned.1.call-start = ((), (), s32[]{:S(2)}) async-start(), calls=%async_computation.11 | async-start | bytes 5750784 | tf_op jit(solution)/shard_map/all_gather | solution.py:37
  20.1 131.2 %copy-start.54 = (f32[6]{0:T(128)}, f32[6]{0:T(128)S(1)}, u32[]{:S(2)}) copy-start(f32[6]{0:T(128)S(1)} %dynamic_slice.36) | copy-start | bytes 76
  39.2 142.6 %all-to-all-start = ((bf16[4,384,384]{1,2,0:T(8,128)(2,1)}), bf16[4,384,384]{1,2,0:T(8,128)(2,1)}, u32[]{:S(2)}, u32[]{:S(2)}) async-start(bf16[4,384,384]{1,2,0:T(8,128)(2,1)} %pad_maximum_fusion.3), calls=%async_computation | async-start | bytes 2359296 | tf_op jit(solution)/shard_map/all_to_all | solution.py:192
  43.5 186.1 %reduce-scatter.9.cloned.1.call-start = ((), (), s32[]{:S(2)}) async-start(), calls=%async_computation.13 | async-start | bytes 3932160 | tf_op jit(solution)/shard_map/reduce_scatter | solution.py:49
  186.7 89.0 %all-gather.26.cloned.1.call-start = ((), (), s32[]{:S(2)}) async-start(), calls=%async_computation.18 | async-start | bytes 3932160 | tf_op jit(solution)/shard_map/all_gather | solution.py:45
  187.8 313.2 %copy-start.48 = (f32[256]{0:T(256)}, f32[256]{0:T(256)S(1)}, u32[]{:S(2)}) copy-start(f32[256]{0:T(256)S(1)} %compare_convert_fusion) | copy-start | bytes 3076
  188.9 127.1 %all-gather.24.cloned.1.call-start = ((), (), s32[]{:S(2)}) async-start(), calls=%async_computation.16 | async-start | bytes 3538944 | tf_op jit(solution)/shard_map/all_gather | solution.py:37
  189.8 192.1 %all-gather.22.cloned.1.call-start = ((), (), s32[]{:S(2)}) async-start(), calls=%async_computation.15 | async-start | bytes 7077888 | tf_op jit(solution)/shard_map/all_gather | solution.py:37
  204.1 222.7 %all-gather.20.cloned.1.call-start = ((), (), s32[]{:S(2)}) async-start(), calls=%async_computation.14 | async-start | bytes 3932160 | tf_op jit(solution)/shard_map/all_gather | solution.py:45
  231.1 269.9 %copy-start.44 = (f32[256]{0:T(256)}, f32[256]{0:T(256)S(1)}, u32[]{:S(2)}) copy-start(f32[256]{0:T(256)S(1)} %fusion.73) | copy-start | bytes 3076
  233.4 265.1 %reduce-scatter.13.cloned.1.call-start = ((), (), s32[]{:S(2)}) async-start(), calls=%async_computation.19 | async-start | bytes 3932160 | tf_op jit(solution)/shard_map/reduce_scatter | solution.py:49
  454.5 93.2 %all-gather.28.cloned.1.call-start = ((), (), s32[]{:S(2)}) async-start(), calls=%async_computation.20 | async-start | bytes 3932160 | tf_op jit(solution)/shard_map/all_gather | solution.py:45
  503.7 104.3 %reduce-scatter.23.cloned.1.call-start = ((), (), s32[]{:S(2)}) async-start(), calls=%async_computation.25 | async-start | bytes 3538944 | tf_op jit(solution)/shard_map/reduce_scatter | solution.py:41
  511.4 150.9 %reduce-scatter.21.cloned.1.call-start = ((), (), s32[]{:S(2)}) async-start(), calls=%async_computation.24 | async-start | bytes 7077888 | tf_op jit(solution)/shard_map/reduce_scatter | solution.py:41
  523.1 198.6 %reduce-scatter.17.cloned.1.call-start = ((), (), s32[]{:S(2)}) async-start(), calls=%async_computation.22 | async-start | bytes 5750784 | tf_op jit(solution)/shard_map/reduce_scatter | solution.py:41
  607.9 144.8 %all-gather.30.cloned.1.call-start = ((), (), s32[]{:S(2)}) async-start(), calls=%async_computation.26 | async-start | bytes 1966080 | tf_op jit(solution)/shard_map/all_gather | solution.py:265
  608.5 179.3 %reduce-scatter.19.cloned.1.call-start = ((), (), s32[]{:S(2)}) async-start(), calls=%async_computation.23 | async-start | bytes 1327104 | tf_op jit(solution)/shard_map/reduce_scatter | solution.py:41
  631.2 200.6 %all-gather.34.cloned.1.call-start = ((), (), s32[]{:S(2)}) async-start(), calls=%async_computation.28 | async-start | bytes 3932160 | tf_op jit(solution)/shard_map/all_gather | solution.py:266
  662.3 216.2 %reduce-scatter.15.cloned.1.call-start = ((), (), s32[]{:S(2)}) async-start(), calls=%async_computation.21 | async-start | bytes 3932160 | tf_op jit(solution)/shard_map/reduce_scatter | solution.py:49
  672.5 253.6 %reduce-scatter.11.cloned.1.call-start = ((), (), s32[]{:S(2)}) async-start(), calls=%async_computation.17 | async-start | bytes 3932160 | tf_op jit(solution)/shard_map/reduce_scatter | solution.py:49
  680.3 286.7 %all-gather.32.cloned.1.call-start = ((), (), s32[]{:S(2)}) async-start(), calls=%async_computation.27 | async-start | bytes 3194880 | tf_op jit(solution)/shard_map/all_gather | solution.py:270
  (67 other events, 946.9 us)
Sparse Core Ops, SparseCore 0:
  10.2 25.4 all-gather.17
  38.2 52.8 all-gather.13
  93.3 54.8 all-gather.15
  186.8 42.6 reduce-scatter.8
  231.8 43.8 all-gather.25
  277.8 38.2 all-gather.23
  318.2 63.5 all-gather.21
  384.3 42.4 all-gather.19
  454.6 43.8 reduce-scatter.12
  503.8 43.8 all-gather.27
  550.6 40.3 reduce-scatter.22
  593.2 69.0 reduce-scatter.20
  664.6 57.0 reduce-scatter.16
  723.4 29.3 all-gather.29
  754.9 32.9 reduce-scatter.18
  789.5 42.1 all-gather.33
  834.6 43.8 reduce-scatter.14
  881.4 44.6 reduce-scatter.10
  927.9 38.9 all-gather.31
